TPU v7x, 32 devices: a whole 2x2x4 slice. The times are simulated.
32 devices in a mesh: expert: 2 (over x), dp: 16 (over z, y, core).
Axes of the slice: x: 2, y: 2, z: 4, core: 2. Of those that a mesh axis runs over, the one named last changes fastest.
Arguments:
- features: bfloat16 [4096, 512], P(('expert', 'dp')), may hold values from -31 to 31
- gradients: bfloat16 [4096, 512], P(('expert', 'dp')), may hold values from -31 to 31
- route_ids: int32 [4096, 2], P(('expert', 'dp')), may hold values from 0 to 7, all different within a row; in each aligned block of 128 rows (0 to 127, 128 to 255, ...) at most 64 rows name the same one
- gate_share: float32 [4096], P(('expert', 'dp')), may hold values from 0.5 to 0.95
- token_mask: int32 [4096], P(('expert', 'dp')), may hold values 0 or 1
- damping: float32 [8, 2, 1], P('expert'), may hold values from 0.5 to 2
Outputs:
- act_inverse: float32 [8, 1, 512, 512], P(None, None, 'dp')
- grad_inverse: float32 [8, 1, 512, 512], P(None, None, 'dp')
Inputs may be any that keep to these rules, and one draw needn't show every extreme that they name: `route_ids`: each token names two different experts. Among the 128 tokens of one device no expert is named by more than 64 tokens, a bound that some block reaches.
All inputs are finite; a program needn't handle non-finite values. Where the computation divides by a largest or mean magnitude, that divisor is 1e-20 or more. No bound on the sum of `token_mask` on one device may be relied on, other than what follows from the above.
Results may differ from a plain program's by a relative error of at most 0.0003.
Values may be sent and summed in bfloat16 or wider, within the bound.
No kernel may reach another device: no remote copies, remote signals or barrier semaphores. Data moves between devices by JAX's collectives and lax.ppermute only.
A program may use at most 64 MiB of HBM per device.

v0:
```python
import functools

import jax
import jax.numpy as jnp
from jax import lax
from jax.experimental import pallas as pl
from jax.experimental.pallas import tpu as pltpu
from jax.sharding import PartitionSpec as P


EXPERTS = 8
TOP = 2
BLOCK = 512
NBLK = 1
CAP = 64
WIDTH = 512
FACTORS = 2 * NBLK
MATRICES = EXPERTS * FACTORS
OWNERS = 2
LANES = 128
TILES = BLOCK // LANES
UPPER = [(top, left) for top in range(TILES) for left in range(top, TILES)]
VMEM_GRANT = 16 * 2**20
COLLECT_GRANT = 60 * 2**20
SENT_SCALE = 2.0**14
AXES = ("expert", "dp")


def whole(*shape):
    return pl.BlockSpec(memory_space=pltpu.VMEM)


META = 8
EARLY = (0, 7,3,6,5)
LATE = (0, 1,2,4,7,3,6,5)


def chip_of(expert_shard, shard, shards):
    chips = shards // FACTORS // OWNERS
    return expert_shard * chips + lax.rem(shard, chips * OWNERS) // OWNERS


def collect_kernel(features, gradients, routes, share, mask, own, sent, ids, weight, kept, sems):
    tokens = features.shape[0]
    lower = lax.axis_index("dp") < lax.axis_size("dp") // FACTORS
    small = [
        pltpu.make_async_copy(routes, ids, sems.at[2]),
        pltpu.make_async_copy(share, weight, sems.at[3]),
        pltpu.make_async_copy(mask, kept, sems.at[4]),
    ]
    for copy in small:
        copy.start()

    def tokens_in(source, target, sem):
        return pltpu.make_async_copy(source, target.at[0:tokens], sems.at[sem])

    @pl.when(lower)
    def _():
        tokens_in(gradients, sent, 0).start()
        tokens_in(features, own, 1).start()

    @pl.when(jnp.logical_not(lower))
    def _():
        tokens_in(features, sent, 0).start()
        tokens_in(gradients, own, 1).start()

    for copy in small:
        copy.wait()
    high = weight[...].astype(jnp.bfloat16).astype(jnp.float32)
    rest = weight[...] - high
    middle = rest.astype(jnp.bfloat16).astype(jnp.float32)
    low = rest - middle
    first = jnp.concatenate(
        [
            ids[0:1, :].astype(jnp.float32),
            ids[1:2, :].astype(jnp.float32),
            kept[...].astype(jnp.float32),
            high,
        ],
        axis=1,
    )
    second = jnp.concatenate([middle, low, jnp.zeros_like(low), jnp.zeros_like(low)], axis=1)
    row = lax.broadcasted_iota(jnp.int32, (META, WIDTH), 0)
    meta = jnp.where(row == 0, first, jnp.where(row == 1, second, 0.0)).astype(jnp.bfloat16)
    own[tokens : tokens + META, :] = meta
    sent[tokens : tokens + META, :] = meta
    tokens_in(features, sent, 0).wait()
    tokens_in(features, own, 1).wait()


def pack_kernel(plan, *refs):
    inputs, outputs = refs[: len(plan)], refs[len(plan) :]
    tokens = inputs[0].shape[0] - META
    shard, shards = lax.axis_index("dp"), lax.axis_size("dp")
    lower = shard < shards // FACTORS
    chip = chip_of(lax.axis_index("expert"), shard, shards)
    expert = lax.broadcasted_iota(jnp.int32, (EXPERTS, tokens), 0)
    earlier = lax.broadcasted_iota(jnp.int32, (tokens, tokens), 0) < lax.broadcasted_iota(
        jnp.int32, (tokens, tokens), 1
    )
    earlier = jnp.where(earlier, 1.0, 0.0).astype(jnp.bfloat16)
    for package, places in zip(inputs, plan):
        slot = lax.broadcasted_iota(jnp.int32, (len(places) * CAP, tokens), 0)
        meta = package[tokens : tokens + META, :].astype(jnp.float32)

        def part(row, index):
            return meta[row : row + 1, index * tokens : (index + 1) * tokens]

        first = part(0, 0).astype(jnp.int32) ^ chip
        second = part(0, 1).astype(jnp.int32) ^ chip
        kept = part(0, 2)
        share = (part(0, 3) + part(1, 0)) + part(1, 1)
        is_first, is_second = expert == first, expert == second
        member = jnp.where(is_first | is_second, 1.0, 0.0).astype(jnp.bfloat16)
        position = jnp.dot(member, earlier, preferred_element_type=jnp.float32)
        wide = package[0:tokens, :].astype(jnp.float32)

        def picked(chosen, named):
            spot = jnp.sum(jnp.where(chosen, position, 0.0), axis=0, keepdims=True)
            base = jnp.full_like(named, -len(places) * CAP - CAP)
            for rank, (apart, _, _) in enumerate(places):
                base = jnp.where(named == apart, rank * CAP, base)
            hit = slot == base + spot.astype(jnp.int32)
            return jnp.where(hit, 1.0, 0.0).astype(jnp.bfloat16)

        def weighted(weight):
            weight = jnp.where(lower, kept, weight * kept)
            column = jnp.transpose(jnp.broadcast_to(weight, (tokens, tokens)))
            column = jnp.concatenate([column] * (WIDTH // tokens), axis=1)
            return (wide * column).astype(jnp.bfloat16)

        picks = jnp.concatenate([picked(is_first, first), picked(is_second, second)], axis=1)
        pairs = jnp.concatenate([weighted(share), weighted(1.0 - share)], axis=0)
        rows = jnp.dot(picks, pairs, preferred_element_type=jnp.float32).astype(jnp.bfloat16)
        for rank, (_, index, row) in enumerate(places):
            outputs[index][row : row + CAP, :] = rows[rank * CAP : (rank + 1) * CAP]


def gram_kernel(*refs):
    rows = jnp.concatenate([ref[...] for ref in refs[:-1]], axis=0)
    gram = lax.dot_general(
        rows, rows, (((0,), (0,)), ((), ())), preferred_element_type=jnp.float32
    )
    for index, (top, left) in enumerate(UPPER):
        refs[-1][index] = gram[
            top * LANES : (top + 1) * LANES, left * LANES : (left + 1) * LANES
        ]


def split(value):
    high = value.astype(jnp.bfloat16)
    return high, (value - high.astype(jnp.float32)).astype(jnp.bfloat16)


def product(left, right):
    (left_high, left_low), (right_high, right_low) = left, right

    def dot(a, b):
        return jnp.dot(a, b, preferred_element_type=jnp.float32)

    return dot(left_high, right_high) + (dot(left_high, right_low) + dot(left_low, right_high))


def newton_kernel(load_inverse, owners, shards, damping, mine, other, out):
    shard = lax.axis_index("dp")
    core = lax.rem(shard, owners)
    factor = shard // (shards // FACTORS)
    expert = lax.rem(shard, shards // FACTORS) // owners
    place = lax.broadcasted_iota(jnp.int32, (BLOCK, BLOCK), 0)
    identity = jnp.where(place == lax.broadcasted_iota(jnp.int32, (BLOCK, BLOCK), 1), 1.0, 0.0)
    tiles = {}
    for index, (top, left) in enumerate(UPPER):
        tiles[top, left] = mine[index] + other[index]
        if top != left:
            tiles[left, top] = jnp.transpose(tiles[top, left])
    gram = jnp.concatenate(
        [
            jnp.concatenate([tiles[top, left] for left in range(TILES)], axis=1)
            for top in range(TILES)
        ],
        axis=0,
    )
    matrix = gram * load_inverse + damping[factor, expert] * identity
    bound = jnp.max(jnp.sum(jnp.abs(matrix), axis=0, keepdims=True), axis=1, keepdims=True)
    scale = 1.0 / bound
    error = identity - scale * matrix
    parts = split(error)
    square = split(product(parts, parts))
    start = (identity + error).reshape(shards // owners, owners, BLOCK // shards, BLOCK)
    rows = start[:, 0]
    for turn in range(1, owners):
        rows = jnp.where(core == turn, start[:, turn], rows)
    rows = rows.reshape(BLOCK // owners, BLOCK)
    rows = rows + product(split(rows), square)
    last = rows + product(split(product(split(rows), square)), square)
    last = (scale * SENT_SCALE) * last
    encode(core, shards, owners, last, out)


def encode(core, shards, owners, rows, out):
    share = BLOCK // shards
    out[...] = rows
    turns = shards // owners
    starts = [turn * owners * share // LANES * LANES for turn in range(turns)]
    tile = jnp.concatenate(
        [
            rows[turn * share : (turn + 1) * share, start : start + LANES]
            for turn, start in enumerate(starts)
        ],
        axis=0,
    )
    place = lax.broadcasted_iota(jnp.int32, tile.shape, 0)
    row = lax.rem(place, share)
    first = lax.rem(place // share * (owners * share), LANES) + core * share
    column = lax.broadcasted_iota(jnp.int32, tile.shape, 1) - first
    high = tile.astype(jnp.bfloat16).astype(jnp.float32)
    low = tile - high
    beside = pltpu.roll(low, LANES - 1, 1)
    tile = jnp.where(column == row, high, tile)
    tile = jnp.where((column == row - 1) & (row > 0), beside, tile)
    tile = jnp.where((column == 0) & (row == 2), pltpu.roll(low, 2, 0), tile)
    for turn, start in enumerate(starts):
        part = slice(turn * share, (turn + 1) * share)
        out[part, start : start + LANES] = tile[part]


def decode_kernel(rows, act, grad):
    groups, share = lax.axis_size("expert"), act.shape[2]
    first = lax.axis_index("dp") * share
    start = pl.multiple_of(first // LANES * LANES, LANES)

    def by_factor(value):
        value = value.reshape(groups, FACTORS, EXPERTS // groups, share, value.shape[-1])
        return (
            (out, value[:, factor].reshape(EXPERTS, share, value.shape[-1]))
            for out, factor in ((act, 0), (grad, 1))
        )

    for out, value in by_factor(rows[...] * (1.0 / SENT_SCALE)):
        out[:, 0] = value
    total = rows.shape[0]
    tile = rows[:, pl.ds(start, LANES)] * (1.0 / SENT_SCALE)
    row = lax.rem(lax.broadcasted_iota(jnp.int32, (total, LANES), 0), share)
    column = lax.broadcasted_iota(jnp.int32, (total, LANES), 1) - (first - start)

    def moved(down, right):
        value = tile
        if down:
            value = pltpu.roll(value, down % total, 0)
        if right:
            value = pltpu.roll(value, right % LANES, 1)
        return value

    fixed = jnp.where(column == row, tile + jnp.where(row > 0, moved(0, 1), moved(-2, 0)), tile)
    fixed = jnp.where((column == row - 1) & (row > 0), moved(1, -1), fixed)
    fixed = jnp.where((column == 0) & (row == 2), moved(2, -2), fixed)
    for out, value in by_factor(fixed):
        out[:, 0, :, pl.ds(start, LANES)] = value


def owned(features, gradients, route_ids, gate_share, token_mask, damping):
    tokens = features.shape[0]
    experts_axis, shards = lax.axis_size("expert"), lax.axis_size("dp")
    devices = experts_axis * shards
    owners = devices // MATRICES
    load_inverse = 1.0 / (tokens * devices * TOP / EXPERTS)
    spec = whole()
    params = pltpu.CompilerParams(vmem_limit_bytes=VMEM_GRANT)
    package = pltpu.VMEM((tokens + META, WIDTH), jnp.bfloat16)
    own, sent = pl.pallas_call(
        collect_kernel,
        out_shape=(package, package),
        in_specs=[pl.BlockSpec(memory_space=pltpu.HBM)] * 5,
        out_specs=(spec, spec),
        scratch_shapes=[
            pltpu.VMEM((TOP, tokens), jnp.int32),
            pltpu.VMEM((1, tokens), jnp.float32),
            pltpu.VMEM((1, tokens), jnp.int32),
            pltpu.SemaphoreType.DMA((5,)),
        ],
        compiler_params=pltpu.CompilerParams(vmem_limit_bytes=COLLECT_GRANT),
        name="collect",
    )(
        features,
        gradients,
        route_ids.T,
        gate_share.reshape(1, tokens),
        token_mask.reshape(1, tokens),
    )
    far = shards // FACTORS
    chips = far // owners

    def pack(packages, wanted):
        plan, sizes = [[] for _ in packages], []
        for index, (apart, sources) in enumerate(wanted):
            for order, source in enumerate(sources):
                plan[source].append((apart, index, order * CAP))
            sizes.append(len(sources) * CAP)
        return pl.pallas_call(
            functools.partial(pack_kernel, plan),
            out_shape=[pltpu.VMEM((size, WIDTH), jnp.bfloat16) for size in sizes],
            in_specs=[spec] * len(packages),
            out_specs=[spec] * len(sizes),
            compiler_params=params,
            name="pack",
        )(*packages)

    def deliver(block, step):
        if step == 0:
            return block
        apart = step // chips * shards + step % chips * owners
        return lax.ppermute(block, AXES, [(i, i ^ apart) for i in range(devices)])

    early = [(step, (0,)) for step in EARLY]
    late = [(step, (1,) if step in EARLY else (0, 1)) for step in LATE]
    got = lax.ppermute(sent, "dp", [(i, (i + far) % shards) for i in range(shards)])
    blocks = pack([own], early)
    received = []
    for block, (step, _) in zip(blocks, early):
        received.append(deliver(block, step))
    blocks = pack([own, got], late)
    for block, (step, _) in zip(blocks, late):
        received.append(deliver(block, step))
    mine = pl.pallas_call(
        gram_kernel,
        out_shape=pltpu.VMEM((len(UPPER), LANES, LANES), jnp.float32),
        in_specs=[spec] * len(received),
        out_specs=spec,
        compiler_params=params,
        name="gram",
    )(*received)
    other = lax.ppermute(mine, "dp", [(i, i ^ 1) for i in range(shards)])
    rows = pl.pallas_call(
        functools.partial(newton_kernel, load_inverse, owners, shards),
        out_shape=pltpu.VMEM((BLOCK // owners, BLOCK), jnp.float32),
        in_specs=[pl.BlockSpec(memory_space=pltpu.SMEM), spec, spec],
        out_specs=spec,
        compiler_params=params,
        name="newton",
    )(damping.reshape(-1, FACTORS).T, mine, other)
    sent = jnp.concatenate([rows.astype(jnp.float16)] * experts_axis, axis=0)
    lanes = range(owners)
    same_core = [
        [e * shards + i + c for e in range(experts_axis) for i in range(0, shards, owners)]
        for c in lanes
    ]
    gathered = lax.all_to_all(
        sent, AXES, split_axis=0, concat_axis=0, tiled=True, axis_index_groups=same_core
    )
    result = jax.ShapeDtypeStruct((EXPERTS, NBLK, BLOCK // shards, BLOCK), jnp.float32)
    return pl.pallas_call(
        decode_kernel,
        out_shape=(result, result),
        in_specs=[spec],
        out_specs=(spec, spec),
        compiler_params=params,
        name="decode",
    )(gathered.astype(jnp.float32))


def slot_table(route_ids, capacity):
    pair_experts = route_ids.reshape(-1)
    onehot = (pair_experts[:, None] == jnp.arange(EXPERTS, dtype=jnp.int32)[None, :]).astype(
        jnp.int32
    )
    running = jnp.cumsum(onehot, axis=0)
    position = jnp.sum(onehot * running, axis=1) - 1
    target = pair_experts * capacity + position
    sources = jnp.arange(1, pair_experts.shape[0] + 1, dtype=jnp.int32)
    return jnp.zeros((EXPERTS * capacity,), jnp.int32).at[target].set(sources)


def newton_rows(rows_now, matrix, whole_now):
    left_product = jnp.einsum("eirk,eikc->eirc", rows_now, matrix, precision=lax.Precision.HIGHEST)
    return 2.0 * rows_now - jnp.einsum(
        "eirk,eikc->eirc", left_product, whole_now, precision=lax.Precision.HIGHEST
    )


def first_iterate(matrix, identity, inverse_bound):
    bound_scale = inverse_bound[:, :, None, None]
    return 2.0 * bound_scale * identity - bound_scale * bound_scale * matrix


def shared(features, gradients, route_ids, gate_share, token_mask, damping):
    tokens_here = features.shape[0]
    capacity = CAP
    blocks = 2 * NBLK
    kept_mask = token_mask.astype(jnp.float32)
    weight_pair = jnp.stack([gate_share, 1.0 - gate_share], axis=1) * kept_mask[:, None]
    kept_rows = features * token_mask.astype(jnp.bfloat16)[:, None]
    pair_grads = (gradients[:, None, :].astype(jnp.float32) * weight_pair[:, :, None]).astype(
        jnp.bfloat16
    )
    repeated = jnp.broadcast_to(kept_rows[:, None, :], pair_grads.shape)
    pair_rows = jnp.concatenate([repeated, pair_grads], axis=2).reshape(
        tokens_here * TOP, 2 * WIDTH
    )
    padded = jnp.concatenate([jnp.zeros((1, 2 * WIDTH), jnp.bfloat16), pair_rows], axis=0)
    buffer = jnp.take(padded, slot_table(route_ids, capacity), axis=0).reshape(
        EXPERTS, capacity, blocks, BLOCK
    )
    load_inverse = 1.0 / (
        tokens_here * lax.axis_size("expert") * lax.axis_size("dp") * TOP / EXPERTS
    )
    received = lax.all_to_all(buffer, "expert", split_axis=0, concat_axis=1, tiled=True)
    gram_blocks = (
        jnp.einsum("erib,eric->eibc", received, received, preferred_element_type=jnp.float32)
        * load_inverse
    )
    damping_flat = damping.reshape(damping.shape[0], blocks)[:, :, None, None]
    rows_share = BLOCK // lax.axis_size("dp")
    row_start = lax.axis_index("dp") * rows_share
    identity = jnp.eye(BLOCK, dtype=jnp.float32)
    summed = lax.psum(gram_blocks, "dp")
    matrix = summed + damping_flat * identity
    largest_sum = jnp.max(jnp.sum(jnp.abs(matrix), axis=3), axis=2)
    inverse_bound = 1.0 / largest_sum
    iterate_one = first_iterate(matrix, identity, inverse_bound)
    iterate_two = newton_rows(iterate_one, matrix, iterate_one)
    second_rows = lax.dynamic_slice_in_dim(iterate_two, row_start, rows_share, 2)
    third_rows = newton_rows(second_rows, matrix, iterate_two)
    act_rows = third_rows[:, :NBLK]
    grad_rows = third_rows[:, NBLK:]
    return (
        lax.all_gather(act_rows, "expert", axis=0, tiled=True),
        lax.all_gather(grad_rows, "expert", axis=0, tiled=True),
    )


def solution(mesh):
    placed = (
        P(("expert", "dp"), None),
        P(("expert", "dp"), None),
        P(("expert", "dp"), None),
        P(("expert", "dp")),
        P(("expert", "dp")),
        P("expert", None, None),
    )
    paired = mesh.shape["expert"] * mesh.shape["dp"] == 2 * MATRICES
    return jax.shard_map(
        owned if paired else shared,
        mesh=mesh,
        in_specs=placed,
        out_specs=(P(None, None, "dp", None), P(None, None, "dp", None)),
        check_vma=False,
    )
```

profile of v0, /device:TPU:0, one launch (start us, length us, event | category | flops | bytes accessed | tf_op | source)
XLA Modules:
  0.0 56.2 jit_solution(14687612152092552388)
XLA Ops:
  0.6 1.1 %collect.1 = (bf16[136,512]{1,0:T(8,128)(2,1)S(1)}, bf16[136,512]{1,0:T(8,128)(2,1)S(1)}) custom-call(bf16[128,512]{1,0:T(8,128)(2,1)} %features.1, bf16[128,512]{1,0:T(8,128)(2,1)} %gradients.1, s32[2,128]{1,0:T(2,128)} %bitcast.12, f32[1,128]{1,0:T(1,128)} %bitcast.13, s32[1,128]{1,0:T(1,128)} %bitcast.14), custom_call_target="tpu_custom_call" | custom-call | tf_op jit(solution)/shard_map/collect/pallas_call | solution.py:270
  1.7 4.1 %collective-permute-start.4 = (bf16[136,512]{1,0:T(8,128)(2,1)S(1)}, bf16[136,512]{1,0:T(8,128)(2,1)S(1)}, u32[]{:S(2)}, u32[]{:S(2)}) collective-permute-start(bf16[136,512]{1,0:T(8,128)(2,1)S(1)} %get-tuple-element.23), channel_id=1, source_target_pairs={{0,8},{1,9},{2,10},{3,11},{4,12},{5,13},{6,14},{7,15},{8,0},{9,1},... | collective-permute-start | bytes 417800 | tf_op jit(solution)/shard_map/ppermute | solution.py:316
  5.8 0.4 pack.2
  6.2 3.5 %collective-permute-start = (bf16[64,512]{1,0:T(8,128)(2,1)S(1)}, bf16[64,512]{1,0:T(8,128)(2,1)S(1)}, u32[]{:S(2)}, u32[]{:S(2)}) collective-permute-start(bf16[64,512]{1,0:T(8,128)(2,1)S(1)} %get-tuple-element.19), channel_id=1, source_target_pairs={{0,22},{1,23},{2,20},{3,21},{4,18},{5,19},{6,16},{7,17},{8,30},{9,... | collective-permute-start | bytes 196616 | tf_op jit(solution)/shard_map/ppermute | solution.py:312
  9.7 0.4 collective-permute-start.1
  10.1 1.5 %collective-permute-start.2 = (bf16[64,512]{1,0:T(8,128)(2,1)S(1)}, bf16[64,512]{1,0:T(8,128)(2,1)S(1)}, u32[]{:S(2)}, u32[]{:S(2)}) collective-permute-start(bf16[64,512]{1,0:T(8,128)(2,1)S(1)} %get-tuple-element.21), channel_id=1, source_target_pairs={{0,20},{1,21},{2,22},{3,23},{4,16},{5,17},{6,18},{7,19},{8,28},{9,... | collective-permute-start | bytes 196616 | tf_op jit(solution)/shard_map/ppermute | solution.py:312
  11.7 2.4 %collective-permute-start.3 = (bf16[64,512]{1,0:T(8,128)(2,1)S(1)}, bf16[64,512]{1,0:T(8,128)(2,1)S(1)}, u32[]{:S(2)}, u32[]{:S(2)}) collective-permute-start(bf16[64,512]{1,0:T(8,128)(2,1)S(1)} %get-tuple-element.22), channel_id=1, source_target_pairs={{0,18},{1,19},{2,16},{3,17},{4,22},{5,23},{6,20},{7,21},{8,26},{9,... | collective-permute-start | bytes 196616 | tf_op jit(solution)/shard_map/ppermute | solution.py:312
  14.1 0.0 collective-permute-done.4.refs_1_
  14.1 0.6 %pack.3 = (bf16[64,512]{1,0:T(8,128)(2,1)S(1)}, bf16[128,512]{1,0:T(8,128)(2,1)S(1)}, bf16[128,512]{1,0:T(8,128)(2,1)S(1)}, bf16[128,512]{1,0:T(8,128)(2,1)S(1)}...) custom-call(bf16[136,512]{1,0:T(8,128)(2,1)S(1)} %get-tuple-element., ...), custom_call_target="tpu_custom_call" | custom-call | tf_op jit(solution)/shard_map/pack/pallas_call | solution.py:299
  14.7 1.1 %collective-permute-start.8 = (bf16[64,512]{1,0:T(8,128)(2,1)S(1)}, bf16[64,512]{1,0:T(8,128)(2,1)S(1)}, u32[]{:S(2)}, u32[]{:S(2)}) collective-permute-start(bf16[64,512]{1,0:T(8,128)(2,1)S(1)} %get-tuple-element.28), channel_id=1, source_target_pairs={{0,22},{1,23},{2,20},{3,21},{4,18},{5,19},{6,16},{7,17},{8,30},{9,... | collective-permute-start | bytes 196616 | tf_op jit(solution)/shard_map/ppermute | solution.py:312
  15.8 0.0 collective-permute-done.refs_1_
  15.8 1.9 %collective-permute-start.9 = (bf16[64,512]{1,0:T(8,128)(2,1)S(1)}, bf16[64,512]{1,0:T(8,128)(2,1)S(1)}, u32[]{:S(2)}, u32[]{:S(2)}) collective-permute-start(bf16[64,512]{1,0:T(8,128)(2,1)S(1)} %get-tuple-element.29), channel_id=1, source_target_pairs={{0,6},{1,7},{2,4},{3,5},{4,2},{5,3},{6,0},{7,1},{8,14},{9,15},{10,... | collective-permute-start | bytes 196616 | tf_op jit(solution)/shard_map/ppermute | solution.py:312
  17.7 0.0 collective-permute-done.1.refs_2_
  17.7 1.0 %collective-permute-start.5 = (bf16[128,512]{1,0:T(8,128)(2,1)S(1)}, bf16[128,512]{1,0:T(8,128)(2,1)S(1)}, u32[]{:S(2)}, u32[]{:S(2)}) collective-permute-start(bf16[128,512]{1,0:T(8,128)(2,1)S(1)} %get-tuple-element.25), channel_id=1, source_target_pairs={{0,2},{1,3},{2,0},{3,1},{4,6},{5,7},{6,4},{7,5},{8,10},{9,11},{10,... | collective-permute-start | bytes 393224 | tf_op jit(solution)/shard_map/ppermute | solution.py:312
  18.7 0.0 collective-permute-done.2.refs_3_
  18.7 0.6 %collective-permute-start.6 = (bf16[128,512]{1,0:T(8,128)(2,1)S(1)}, bf16[128,512]{1,0:T(8,128)(2,1)S(1)}, u32[]{:S(2)}, u32[]{:S(2)}) collective-permute-start(bf16[128,512]{1,0:T(8,128)(2,1)S(1)} %get-tuple-element.26), channel_id=1, source_target_pairs={{0,4},{1,5},{2,6},{3,7},{4,0},{5,1},{6,2},{7,3},{8,12},{9,13},{10,... | collective-permute-start | bytes 393224 | tf_op jit(solution)/shard_map/ppermute | solution.py:312
  19.3 0.0 collective-permute-done.3.refs_4_
  19.3 0.8 %collective-permute-start.7 = (bf16[128,512]{1,0:T(8,128)(2,1)S(1)}, bf16[128,512]{1,0:T(8,128)(2,1)S(1)}, u32[]{:S(2)}, u32[]{:S(2)}) collective-permute-start(bf16[128,512]{1,0:T(8,128)(2,1)S(1)} %get-tuple-element.27), channel_id=1, source_target_pairs={{0,16},{1,17},{2,18},{3,19},{4,20},{5,21},{6,22},{7,23},{8,24},{9,... | collective-permute-start | bytes 393224 | tf_op jit(solution)/shard_map/ppermute | solution.py:312
  20.2 1.3 %collective-permute-done.8.refs_9_ = bf16[64,512]{1,0:T(8,128)(2,1)S(1)} collective-permute-done((bf16[64,512]{1,0:T(8,128)(2,1)S(1)}, bf16[64,512]{1,0:T(8,128)(2,1)S(1)}, u32[]{:S(2)}, u32[]{:S(2)}) %collective-permute-start.8) | collective-permute-done | bytes 65568 | tf_op jit(solution)/shard_map/ppermute | solution.py:312
  21.5 0.7 %collective-permute-start.10 = (bf16[64,512]{1,0:T(8,128)(2,1)S(1)}, bf16[64,512]{1,0:T(8,128)(2,1)S(1)}, u32[]{:S(2)}, u32[]{:S(2)}) collective-permute-start(bf16[64,512]{1,0:T(8,128)(2,1)S(1)} %get-tuple-element.30), channel_id=1, source_target_pairs={{0,20},{1,21},{2,22},{3,23},{4,16},{5,17},{6,18},{7,19},{8,28},{9,... | collective-permute-start | bytes 196616 | tf_op jit(solution)/shard_map/ppermute | solution.py:312
  22.2 0.0 collective-permute-done.9.refs_10_
  22.2 2.0 %collective-permute-start.11 = (bf16[64,512]{1,0:T(8,128)(2,1)S(1)}, bf16[64,512]{1,0:T(8,128)(2,1)S(1)}, u32[]{:S(2)}, u32[]{:S(2)}) collective-permute-start(bf16[64,512]{1,0:T(8,128)(2,1)S(1)} %get-tuple-element.31), channel_id=1, source_target_pairs={{0,18},{1,19},{2,16},{3,17},{4,22},{5,23},{6,20},{7,21},{8,26},{9,... | collective-permute-start | bytes 196616 | tf_op jit(solution)/shard_map/ppermute | solution.py:312
  24.2 2.5 %collective-permute-done.10.refs_11_ = bf16[64,512]{1,0:T(8,128)(2,1)S(1)} collective-permute-done((bf16[64,512]{1,0:T(8,128)(2,1)S(1)}, bf16[64,512]{1,0:T(8,128)(2,1)S(1)}, u32[]{:S(2)}, u32[]{:S(2)}) %collective-permute-start.10) | collective-permute-done | bytes 65568 | tf_op jit(solution)/shard_map/ppermute | solution.py:312
  26.7 0.7 %collective-permute-done.11.refs_12_ = bf16[64,512]{1,0:T(8,128)(2,1)S(1)} collective-permute-done((bf16[64,512]{1,0:T(8,128)(2,1)S(1)}, bf16[64,512]{1,0:T(8,128)(2,1)S(1)}, u32[]{:S(2)}, u32[]{:S(2)}) %collective-permute-start.11) | collective-permute-done | bytes 65568 | tf_op jit(solution)/shard_map/ppermute | solution.py:312
  27.4 0.0 collective-permute-done.5.refs_6_
  27.4 0.0 collective-permute-done.6.refs_7_
  27.4 0.0 collective-permute-done.7.refs_8_
  27.4 0.7 %gram.1.mine = f32[10,128,128]{2,1,0:T(8,128)S(1)} custom-call(bf16[64,512]{1,0:T(8,128)(2,1)S(1)} %get-tuple-element.18.refs_0_, bf16[64,512]{1,0:T(8,128)(2,1)S(1)} %collective-permute-done.refs_1_, bf16[64,512]{1,0:T(8,128)(2,1)S(1)} %collective-permute-done.1.refs_2_, bf16[64,512]{1,0:T(8,128)(2,1)S(1)} %collective-permute-done.2.refs_3_, ...), custom_call_target="tpu_custom_call" | custom-call | tf_op jit(solution)/shard_map/gram/pallas_call | solution.py:324
  28.1 0.0 copy-start
  28.1 0.1 collective-permute-start.12
  28.2 2.1 %collective-permute-done.12.other = f32[10,128,128]{2,1,0:T(8,128)S(1)} collective-permute-done((f32[10,128,128]{2,1,0:T(8,128)S(1)}, f32[10,128,128]{2,1,0:T(8,128)S(1)}, u32[]{:S(2)}, u32[]{:S(2)}) %collective-permute-start.12) | collective-permute-done | bytes 655392 | tf_op jit(solution)/shard_map/ppermute | solution.py:332
  30.3 0.0 copy-done
  30.3 3.5 %newton.1 = f32[256,512]{1,0:T(8,128)S(1)} custom-call(f32[2,4]{1,0:T(2,128)S(1)} %bitcast.10, f32[10,128,128]{2,1,0:T(8,128)S(1)} %gram.1.mine, f32[10,128,128]{2,1,0:T(8,128)S(1)} %collective-permute-done.12.other), custom_call_target="tpu_custom_call" | custom-call | tf_op jit(solution)/shard_map/newton/pallas_call | solution.py:333
  33.8 0.1 pad_maximum_fusion
  34.0 20.8 %all_to_all.9 = f16[16,32,512]{2,1,0:T(8,128)(2,1)S(1)} all-to-all(f16[16,32,512]{2,1,0:T(8,128)(2,1)S(1)} %bitcast.11), channel_id=1, replica_groups={{0,2,4,6,8,10,12,14,16,18,20,22,24,26,28,30},{1,3,5,7,9,11,13,15,17,19,..., dimensions={0} | all-to-all | bytes 1048576 | tf_op jit(solution)/shard_map/all_to_all | solution.py:347
  54.8 0.2 bitcast_convert_fusion.rows
  55.0 1.2 %decode.1 = (f32[8,1,32,512]{3,2,1,0:T(8,128)}, f32[8,1,32,512]{3,2,1,0:T(8,128)}) custom-call(f32[512,512]{1,0:T(8,128)S(1)} %bitcast_convert_fusion.rows), custom_call_target="tpu_custom_call" | custom-call | tf_op jit(solution)/shard_map/decode/pallas_call | solution.py:351
  (1 shorter events, 0.0 us)
Async XLA Ops:
  1.7 12.4 %collective-permute-start.4 = (bf16[136,512]{1,0:T(8,128)(2,1)S(1)}, bf16[136,512]{1,0:T(8,128)(2,1)S(1)}, u32[]{:S(2)}, u32[]{:S(2)}) collective-permute-start(bf16[136,512]{1,0:T(8,128)(2,1)S(1)} %get-tuple-element.23), channel_id=1, source_target_pairs={{0,8},{1,9},{2,10},{3,11},{4,12},{5,13},{6,14},{7,15},{8,0},{9,1},... | collective-permute-start | bytes 417800 | tf_op jit(solution)/shard_map/ppermute | solution.py:316
  6.2 9.6 %collective-permute-start = (bf16[64,512]{1,0:T(8,128)(2,1)S(1)}, bf16[64,512]{1,0:T(8,128)(2,1)S(1)}, u32[]{:S(2)}, u32[]{:S(2)}) collective-permute-start(bf16[64,512]{1,0:T(8,128)(2,1)S(1)} %get-tuple-element.19), channel_id=1, source_target_pairs={{0,22},{1,23},{2,20},{3,21},{4,18},{5,19},{6,16},{7,17},{8,30},{9,... | collective-permute-start | bytes 196616 | tf_op jit(solution)/shard_map/ppermute | solution.py:312
  9.7 8.0 %collective-permute-start.1 = (bf16[64,512]{1,0:T(8,128)(2,1)S(1)}, bf16[64,512]{1,0:T(8,128)(2,1)S(1)}, u32[]{:S(2)}, u32[]{:S(2)}) collective-permute-start(bf16[64,512]{1,0:T(8,128)(2,1)S(1)} %get-tuple-element.20), channel_id=1, source_target_pairs={{0,6},{1,7},{2,4},{3,5},{4,2},{5,3},{6,0},{7,1},{8,14},{9,15},{10,... | collective-permute-start | bytes 196616 | tf_op jit(solution)/shard_map/ppermute | solution.py:312
  10.1 8.6 %collective-permute-start.2 = (bf16[64,512]{1,0:T(8,128)(2,1)S(1)}, bf16[64,512]{1,0:T(8,128)(2,1)S(1)}, u32[]{:S(2)}, u32[]{:S(2)}) collective-permute-start(bf16[64,512]{1,0:T(8,128)(2,1)S(1)} %get-tuple-element.21), channel_id=1, source_target_pairs={{0,20},{1,21},{2,22},{3,23},{4,16},{5,17},{6,18},{7,19},{8,28},{9,... | collective-permute-start | bytes 196616 | tf_op jit(solution)/shard_map/ppermute | solution.py:312
  11.7 7.7 %collective-permute-start.3 = (bf16[64,512]{1,0:T(8,128)(2,1)S(1)}, bf16[64,512]{1,0:T(8,128)(2,1)S(1)}, u32[]{:S(2)}, u32[]{:S(2)}) collective-permute-start(bf16[64,512]{1,0:T(8,128)(2,1)S(1)} %get-tuple-element.22), channel_id=1, source_target_pairs={{0,18},{1,19},{2,16},{3,17},{4,22},{5,23},{6,20},{7,21},{8,26},{9,... | collective-permute-start | bytes 196616 | tf_op jit(solution)/shard_map/ppermute | solution.py:312
  14.7 6.7 %collective-permute-start.8 = (bf16[64,512]{1,0:T(8,128)(2,1)S(1)}, bf16[64,512]{1,0:T(8,128)(2,1)S(1)}, u32[]{:S(2)}, u32[]{:S(2)}) collective-permute-start(bf16[64,512]{1,0:T(8,128)(2,1)S(1)} %get-tuple-element.28), channel_id=1, source_target_pairs={{0,22},{1,23},{2,20},{3,21},{4,18},{5,19},{6,16},{7,17},{8,30},{9,... | collective-permute-start | bytes 196616 | tf_op jit(solution)/shard_map/ppermute | solution.py:312
  15.8 6.4 %collective-permute-start.9 = (bf16[64,512]{1,0:T(8,128)(2,1)S(1)}, bf16[64,512]{1,0:T(8,128)(2,1)S(1)}, u32[]{:S(2)}, u32[]{:S(2)}) collective-permute-start(bf16[64,512]{1,0:T(8,128)(2,1)S(1)} %get-tuple-element.29), channel_id=1, source_target_pairs={{0,6},{1,7},{2,4},{3,5},{4,2},{5,3},{6,0},{7,1},{8,14},{9,15},{10,... | collective-permute-start | bytes 196616 | tf_op jit(solution)/shard_map/ppermute | solution.py:312
  17.7 9.7 %collective-permute-start.5 = (bf16[128,512]{1,0:T(8,128)(2,1)S(1)}, bf16[128,512]{1,0:T(8,128)(2,1)S(1)}, u32[]{:S(2)}, u32[]{:S(2)}) collective-permute-start(bf16[128,512]{1,0:T(8,128)(2,1)S(1)} %get-tuple-element.25), channel_id=1, source_target_pairs={{0,2},{1,3},{2,0},{3,1},{4,6},{5,7},{6,4},{7,5},{8,10},{9,11},{10,... | collective-permute-start | bytes 393224 | tf_op jit(solution)/shard_map/ppermute | solution.py:312
  18.7 8.7 %collective-permute-start.6 = (bf16[128,512]{1,0:T(8,128)(2,1)S(1)}, bf16[128,512]{1,0:T(8,128)(2,1)S(1)}, u32[]{:S(2)}, u32[]{:S(2)}) collective-permute-start(bf16[128,512]{1,0:T(8,128)(2,1)S(1)} %get-tuple-element.26), channel_id=1, source_target_pairs={{0,4},{1,5},{2,6},{3,7},{4,0},{5,1},{6,2},{7,3},{8,12},{9,13},{10,... | collective-permute-start | bytes 393224 | tf_op jit(solution)/shard_map/ppermute | solution.py:312
  19.3 8.1 %collective-permute-start.7 = (bf16[128,512]{1,0:T(8,128)(2,1)S(1)}, bf16[128,512]{1,0:T(8,128)(2,1)S(1)}, u32[]{:S(2)}, u32[]{:S(2)}) collective-permute-start(bf16[128,512]{1,0:T(8,128)(2,1)S(1)} %get-tuple-element.27), channel_id=1, source_target_pairs={{0,16},{1,17},{2,18},{3,19},{4,20},{5,21},{6,22},{7,23},{8,24},{9,... | collective-permute-start | bytes 393224 | tf_op jit(solution)/shard_map/ppermute | solution.py:312
  21.5 5.2 %collective-permute-start.10 = (bf16[64,512]{1,0:T(8,128)(2,1)S(1)}, bf16[64,512]{1,0:T(8,128)(2,1)S(1)}, u32[]{:S(2)}, u32[]{:S(2)}) collective-permute-start(bf16[64,512]{1,0:T(8,128)(2,1)S(1)} %get-tuple-element.30), channel_id=1, source_target_pairs={{0,20},{1,21},{2,22},{3,23},{4,16},{5,17},{6,18},{7,19},{8,28},{9,... | collective-permute-start | bytes 196616 | tf_op jit(solution)/shard_map/ppermute | solution.py:312
  22.2 5.2 %collective-permute-start.11 = (bf16[64,512]{1,0:T(8,128)(2,1)S(1)}, bf16[64,512]{1,0:T(8,128)(2,1)S(1)}, u32[]{:S(2)}, u32[]{:S(2)}) collective-permute-start(bf16[64,512]{1,0:T(8,128)(2,1)S(1)} %get-tuple-element.31), channel_id=1, source_target_pairs={{0,18},{1,19},{2,16},{3,17},{4,22},{5,23},{6,20},{7,21},{8,26},{9,... | collective-permute-start | bytes 196616 | tf_op jit(solution)/shard_map/ppermute | solution.py:312
  28.1 2.2 %copy-start = (f32[4,2,1]{0,2,1:T(1,128)S(1)}, f32[4,2,1]{0,2,1:T(1,128)}, u32[]{:S(2)}) copy-start(f32[4,2,1]{0,2,1:T(1,128)} %param.11) | copy-start | bytes 100
  28.1 2.2 %collective-permute-start.12 = (f32[10,128,128]{2,1,0:T(8,128)S(1)}, f32[10,128,128]{2,1,0:T(8,128)S(1)}, u32[]{:S(2)}, u32[]{:S(2)}) collective-permute-start(f32[10,128,128]{2,1,0:T(8,128)S(1)} %gram.1.mine), channel_id=1, source_target_pairs={{0,1},{1,0},{2,3},{3,2},{4,5},{5,4},{6,7},{7,6},{8,9},{9,8},{10,11... | collective-permute-start | bytes 1966088 | tf_op jit(solution)/shard_map/ppermute | solution.py:332
where the time goes:
time: 56.4 us; the launch traced here: 56.2 us
  blocking collectives  20.8 us (37%)
  starting transfers between devices  20.2 us (36%)
  Pallas kernels  7.51 us (13%)
  waiting for transfers between devices  6.59 us (12%)
  between operations  0.72 us (1%)
    all_to_all x1, blocking collectives, owned(): lax.all_to_all(sent, AXES, split_axis=0, concat_axis=0, tiled=True, axis_...  20.8 us
    ppermute x11, starting transfers between devices, deliver(): return lax.ppermute(block, AXES, [(i, i ^ apart) for i in range(devices)])  16 us
    ppermute x11, waiting for transfers between devices, deliver(): return lax.ppermute(block, AXES, [(i, i ^ apart) for i in range(devices)])  4.51 us
    ppermute x1, starting transfers between devices, owned(): lax.ppermute(sent, 'dp', [(i, (i + far) % shards) for i in range(shards)])  4.13 us
    pallas_call x1, Pallas kernels, owned(): pl.pallas_call(functools.partial(newton_kernel, load_inverse, owners, sha...  3.49 us
    ppermute x1, waiting for transfers between devices, owned(): other = lax.ppermute(mine, 'dp', [(i, i ^ 1) for i in range(shards)])  2.08 us
    pallas_call x1, Pallas kernels, owned(): pl.pallas_call(decode_kernel, out_shape=(result, result), in_specs=[spec]...  1.24 us
  transfers between devices with their start and end apart: 13, of which 4 were waited for; matrix products, arithmetic and copies ran while one was open for 0% of the time, Pallas kernels for 2%

commit v1 on v0

--- a/solution.py
+++ b/solution.py
@@ -31,8 +31,8 @@
 
 
 META = 8
-EARLY = (0, 7,3,6,5)
-LATE = (0, 1,2,4,7,3,6,5)
+EARLY = (0, 7, 3, 6, 5)
+LATE = (0, 1, 2, 4, 7, 3, 6, 5)
 
 
 def chip_of(expert_shard, shard, shards):
@@ -185,7 +185,9 @@
     scale = 1.0 / bound
     error = identity - scale * matrix
     parts = split(error)
-    square = split(product(parts, parts))
+    cross = jnp.dot(parts[0], parts[1], preferred_element_type=jnp.float32)
+    square = jnp.dot(parts[0], parts[0], preferred_element_type=jnp.float32)
+    square = split(square + (cross + jnp.transpose(cross)))
     start = (identity + error).reshape(shards // owners, owners, BLOCK // shards, BLOCK)
     rows = start[:, 0]
     for turn in range(1, owners):
@@ -224,22 +226,12 @@
         out[part, start : start + LANES] = tile[part]
 
 
-def decode_kernel(rows, act, grad):
+def decode_kernel(rows, act, grad, results, sems):
     groups, share = lax.axis_size("expert"), act.shape[2]
     first = lax.axis_index("dp") * share
     start = pl.multiple_of(first // LANES * LANES, LANES)
-
-    def by_factor(value):
-        value = value.reshape(groups, FACTORS, EXPERTS // groups, share, value.shape[-1])
-        return (
-            (out, value[:, factor].reshape(EXPERTS, share, value.shape[-1]))
-            for out, factor in ((act, 0), (grad, 1))
-        )
-
-    for out, value in by_factor(rows[...] * (1.0 / SENT_SCALE)):
-        out[:, 0] = value
     total = rows.shape[0]
-    tile = rows[:, pl.ds(start, LANES)] * (1.0 / SENT_SCALE)
+    tile = rows[:, pl.ds(start, LANES)]
     row = lax.rem(lax.broadcasted_iota(jnp.int32, (total, LANES), 0), share)
     column = lax.broadcasted_iota(jnp.int32, (total, LANES), 1) - (first - start)
 
@@ -254,8 +246,19 @@
     fixed = jnp.where(column == row, tile + jnp.where(row > 0, moved(0, 1), moved(-2, 0)), tile)
     fixed = jnp.where((column == row - 1) & (row > 0), moved(1, -1), fixed)
     fixed = jnp.where((column == 0) & (row == 2), moved(2, -2), fixed)
-    for out, value in by_factor(fixed):
-        out[:, 0, :, pl.ds(start, LANES)] = value
+
+    def of_factor(value, factor):
+        value = value.reshape(groups, FACTORS, EXPERTS // groups, share, value.shape[-1])
+        return value[:, factor].reshape(EXPERTS, share, value.shape[-1])
+
+    copies = []
+    for factor, out in ((0, act), (1, grad)):
+        results[factor] = of_factor(rows[...], factor)
+        results[factor, :, :, pl.ds(start, LANES)] = of_factor(fixed, factor)
+        copies.append(pltpu.make_async_copy(results.at[factor], out.at[:, 0], sems.at[factor]))
+        copies[-1].start()
+    for copy in copies:
+        copy.wait()
 
 
 def owned(features, gradients, route_ids, gate_share, token_mask, damping):
@@ -352,10 +355,14 @@
         decode_kernel,
         out_shape=(result, result),
         in_specs=[spec],
-        out_specs=(spec, spec),
+        out_specs=(pl.BlockSpec(memory_space=pltpu.HBM),) * FACTORS,
+        scratch_shapes=[
+            pltpu.VMEM((FACTORS, EXPERTS, BLOCK // shards, BLOCK), jnp.float32),
+            pltpu.SemaphoreType.DMA((FACTORS,)),
+        ],
         compiler_params=params,
         name="decode",
-    )(gathered.astype(jnp.float32))
+    )(gathered.astype(jnp.float32) * (1.0 / SENT_SCALE))
 
 
 def slot_table(route_ids, capacity):

time: 56.4 us -> 56.2 us (level)
  no operation moved by 1% of the time
where the time goes in v1:
time: 56.2 us; the launch traced here: 56 us
  blocking collectives  20.8 us (37%)
  starting transfers between devices  20.2 us (36%)
  Pallas kernels  7.29 us (13%)
  waiting for transfers between devices  6.59 us (12%)
  between operations  0.72 us (1%)
    all_to_all x1, blocking collectives, owned(): lax.all_to_all(sent, AXES, split_axis=0, concat_axis=0, tiled=True, axis_...  20.8 us
    ppermute x11, starting transfers between devices, deliver(): return lax.ppermute(block, AXES, [(i, i ^ apart) for i in range(devices)])  16 us
    ppermute x11, waiting for transfers between devices, deliver(): return lax.ppermute(block, AXES, [(i, i ^ apart) for i in range(devices)])  4.51 us
    ppermute x1, starting transfers between devices, owned(): lax.ppermute(sent, 'dp', [(i, (i + far) % shards) for i in range(shards)])  4.13 us
    pallas_call x1, Pallas kernels, owned(): pl.pallas_call(functools.partial(newton_kernel, load_inverse, owners, sha...  3.3 us
    ppermute x1, waiting for transfers between devices, owned(): other = lax.ppermute(mine, 'dp', [(i, i ^ 1) for i in range(shards)])  2.08 us
    pallas_call x1, Pallas kernels, owned(): pl.pallas_call(decode_kernel, out_shape=(result, result), in_specs=[spec]...  1.22 us
  transfers between devices with their start and end apart: 13, of which 4 were waited for; matrix products, arithmetic and copies ran while one was open for 0% of the time, Pallas kernels for 2%

profile of v1, /device:TPU:0, one launch (start us, length us, event | category | flops | bytes accessed | tf_op | source)
XLA Modules:
  0.0 56.0 jit_solution(17012147763169802883)
XLA Ops:
  0.6 1.1 %collect.1 = (bf16[136,512]{1,0:T(8,128)(2,1)S(1)}, bf16[136,512]{1,0:T(8,128)(2,1)S(1)}) custom-call(bf16[128,512]{1,0:T(8,128)(2,1)} %features.1, bf16[128,512]{1,0:T(8,128)(2,1)} %gradients.1, s32[2,128]{1,0:T(2,128)} %bitcast.11, f32[1,128]{1,0:T(1,128)} %bitcast.12, s32[1,128]{1,0:T(1,128)} %bitcast.13), custom_call_target="tpu_custom_call" | custom-call | tf_op jit(solution)/shard_map/collect/pallas_call | solution.py:273
  1.7 4.1 %collective-permute-start.4 = (bf16[136,512]{1,0:T(8,128)(2,1)S(1)}, bf16[136,512]{1,0:T(8,128)(2,1)S(1)}, u32[]{:S(2)}, u32[]{:S(2)}) collective-permute-start(bf16[136,512]{1,0:T(8,128)(2,1)S(1)} %get-tuple-element.23), channel_id=1, source_target_pairs={{0,8},{1,9},{2,10},{3,11},{4,12},{5,13},{6,14},{7,15},{8,0},{9,1},... | collective-permute-start | bytes 417800 | tf_op jit(solution)/shard_map/ppermute | solution.py:319
  5.8 0.4 pack.2
  6.2 3.5 %collective-permute-start = (bf16[64,512]{1,0:T(8,128)(2,1)S(1)}, bf16[64,512]{1,0:T(8,128)(2,1)S(1)}, u32[]{:S(2)}, u32[]{:S(2)}) collective-permute-start(bf16[64,512]{1,0:T(8,128)(2,1)S(1)} %get-tuple-element.19), channel_id=1, source_target_pairs={{0,22},{1,23},{2,20},{3,21},{4,18},{5,19},{6,16},{7,17},{8,30},{9,... | collective-permute-start | bytes 196616 | tf_op jit(solution)/shard_map/ppermute | solution.py:315
  9.7 0.4 collective-permute-start.1
  10.1 1.5 %collective-permute-start.2 = (bf16[64,512]{1,0:T(8,128)(2,1)S(1)}, bf16[64,512]{1,0:T(8,128)(2,1)S(1)}, u32[]{:S(2)}, u32[]{:S(2)}) collective-permute-start(bf16[64,512]{1,0:T(8,128)(2,1)S(1)} %get-tuple-element.21), channel_id=1, source_target_pairs={{0,20},{1,21},{2,22},{3,23},{4,16},{5,17},{6,18},{7,19},{8,28},{9,... | collective-permute-start | bytes 196616 | tf_op jit(solution)/shard_map/ppermute | solution.py:315
  11.7 2.4 %collective-permute-start.3 = (bf16[64,512]{1,0:T(8,128)(2,1)S(1)}, bf16[64,512]{1,0:T(8,128)(2,1)S(1)}, u32[]{:S(2)}, u32[]{:S(2)}) collective-permute-start(bf16[64,512]{1,0:T(8,128)(2,1)S(1)} %get-tuple-element.22), channel_id=1, source_target_pairs={{0,18},{1,19},{2,16},{3,17},{4,22},{5,23},{6,20},{7,21},{8,26},{9,... | collective-permute-start | bytes 196616 | tf_op jit(solution)/shard_map/ppermute | solution.py:315
  14.1 0.0 collective-permute-done.4.refs_1_
  14.1 0.6 %pack.3 = (bf16[64,512]{1,0:T(8,128)(2,1)S(1)}, bf16[128,512]{1,0:T(8,128)(2,1)S(1)}, bf16[128,512]{1,0:T(8,128)(2,1)S(1)}, bf16[128,512]{1,0:T(8,128)(2,1)S(1)}...) custom-call(bf16[136,512]{1,0:T(8,128)(2,1)S(1)} %get-tuple-element., ...), custom_call_target="tpu_custom_call" | custom-call | tf_op jit(solution)/shard_map/pack/pallas_call | solution.py:302
  14.7 1.1 %collective-permute-start.8 = (bf16[64,512]{1,0:T(8,128)(2,1)S(1)}, bf16[64,512]{1,0:T(8,128)(2,1)S(1)}, u32[]{:S(2)}, u32[]{:S(2)}) collective-permute-start(bf16[64,512]{1,0:T(8,128)(2,1)S(1)} %get-tuple-element.28), channel_id=1, source_target_pairs={{0,22},{1,23},{2,20},{3,21},{4,18},{5,19},{6,16},{7,17},{8,30},{9,... | collective-permute-start | bytes 196616 | tf_op jit(solution)/shard_map/ppermute | solution.py:315
  15.8 0.0 collective-permute-done.refs_1_
  15.8 1.9 %collective-permute-start.9 = (bf16[64,512]{1,0:T(8,128)(2,1)S(1)}, bf16[64,512]{1,0:T(8,128)(2,1)S(1)}, u32[]{:S(2)}, u32[]{:S(2)}) collective-permute-start(bf16[64,512]{1,0:T(8,128)(2,1)S(1)} %get-tuple-element.29), channel_id=1, source_target_pairs={{0,6},{1,7},{2,4},{3,5},{4,2},{5,3},{6,0},{7,1},{8,14},{9,15},{10,... | collective-permute-start | bytes 196616 | tf_op jit(solution)/shard_map/ppermute | solution.py:315
  17.7 0.0 collective-permute-done.1.refs_2_
  17.7 1.0 %collective-permute-start.5 = (bf16[128,512]{1,0:T(8,128)(2,1)S(1)}, bf16[128,512]{1,0:T(8,128)(2,1)S(1)}, u32[]{:S(2)}, u32[]{:S(2)}) collective-permute-start(bf16[128,512]{1,0:T(8,128)(2,1)S(1)} %get-tuple-element.25), channel_id=1, source_target_pairs={{0,2},{1,3},{2,0},{3,1},{4,6},{5,7},{6,4},{7,5},{8,10},{9,11},{10,... | collective-permute-start | bytes 393224 | tf_op jit(solution)/shard_map/ppermute | solution.py:315
  18.7 0.0 collective-permute-done.2.refs_3_
  18.7 0.6 %collective-permute-start.6 = (bf16[128,512]{1,0:T(8,128)(2,1)S(1)}, bf16[128,512]{1,0:T(8,128)(2,1)S(1)}, u32[]{:S(2)}, u32[]{:S(2)}) collective-permute-start(bf16[128,512]{1,0:T(8,128)(2,1)S(1)} %get-tuple-element.26), channel_id=1, source_target_pairs={{0,4},{1,5},{2,6},{3,7},{4,0},{5,1},{6,2},{7,3},{8,12},{9,13},{10,... | collective-permute-start | bytes 393224 | tf_op jit(solution)/shard_map/ppermute | solution.py:315
  19.3 0.0 collective-permute-done.3.refs_4_
  19.3 0.8 %collective-permute-start.7 = (bf16[128,512]{1,0:T(8,128)(2,1)S(1)}, bf16[128,512]{1,0:T(8,128)(2,1)S(1)}, u32[]{:S(2)}, u32[]{:S(2)}) collective-permute-start(bf16[128,512]{1,0:T(8,128)(2,1)S(1)} %get-tuple-element.27), channel_id=1, source_target_pairs={{0,16},{1,17},{2,18},{3,19},{4,20},{5,21},{6,22},{7,23},{8,24},{9,... | collective-permute-start | bytes 393224 | tf_op jit(solution)/shard_map/ppermute | solution.py:315
  20.2 1.3 %collective-permute-done.8.refs_9_ = bf16[64,512]{1,0:T(8,128)(2,1)S(1)} collective-permute-done((bf16[64,512]{1,0:T(8,128)(2,1)S(1)}, bf16[64,512]{1,0:T(8,128)(2,1)S(1)}, u32[]{:S(2)}, u32[]{:S(2)}) %collective-permute-start.8) | collective-permute-done | bytes 65568 | tf_op jit(solution)/shard_map/ppermute | solution.py:315
  21.5 0.7 %collective-permute-start.10 = (bf16[64,512]{1,0:T(8,128)(2,1)S(1)}, bf16[64,512]{1,0:T(8,128)(2,1)S(1)}, u32[]{:S(2)}, u32[]{:S(2)}) collective-permute-start(bf16[64,512]{1,0:T(8,128)(2,1)S(1)} %get-tuple-element.30), channel_id=1, source_target_pairs={{0,20},{1,21},{2,22},{3,23},{4,16},{5,17},{6,18},{7,19},{8,28},{9,... | collective-permute-start | bytes 196616 | tf_op jit(solution)/shard_map/ppermute | solution.py:315
  22.2 0.0 collective-permute-done.9.refs_10_
  22.2 2.0 %collective-permute-start.11 = (bf16[64,512]{1,0:T(8,128)(2,1)S(1)}, bf16[64,512]{1,0:T(8,128)(2,1)S(1)}, u32[]{:S(2)}, u32[]{:S(2)}) collective-permute-start(bf16[64,512]{1,0:T(8,128)(2,1)S(1)} %get-tuple-element.31), channel_id=1, source_target_pairs={{0,18},{1,19},{2,16},{3,17},{4,22},{5,23},{6,20},{7,21},{8,26},{9,... | collective-permute-start | bytes 196616 | tf_op jit(solution)/shard_map/ppermute | solution.py:315
  24.2 2.5 %collective-permute-done.10.refs_11_ = bf16[64,512]{1,0:T(8,128)(2,1)S(1)} collective-permute-done((bf16[64,512]{1,0:T(8,128)(2,1)S(1)}, bf16[64,512]{1,0:T(8,128)(2,1)S(1)}, u32[]{:S(2)}, u32[]{:S(2)}) %collective-permute-start.10) | collective-permute-done | bytes 65568 | tf_op jit(solution)/shard_map/ppermute | solution.py:315
  26.7 0.7 %collective-permute-done.11.refs_12_ = bf16[64,512]{1,0:T(8,128)(2,1)S(1)} collective-permute-done((bf16[64,512]{1,0:T(8,128)(2,1)S(1)}, bf16[64,512]{1,0:T(8,128)(2,1)S(1)}, u32[]{:S(2)}, u32[]{:S(2)}) %collective-permute-start.11) | collective-permute-done | bytes 65568 | tf_op jit(solution)/shard_map/ppermute | solution.py:315
  27.4 0.0 collective-permute-done.5.refs_6_
  27.4 0.0 collective-permute-done.6.refs_7_
  27.4 0.0 collective-permute-done.7.refs_8_
  27.4 0.7 %gram.1.mine = f32[10,128,128]{2,1,0:T(8,128)S(1)} custom-call(bf16[64,512]{1,0:T(8,128)(2,1)S(1)} %get-tuple-element.18.refs_0_, bf16[64,512]{1,0:T(8,128)(2,1)S(1)} %collective-permute-done.refs_1_, bf16[64,512]{1,0:T(8,128)(2,1)S(1)} %collective-permute-done.1.refs_2_, bf16[64,512]{1,0:T(8,128)(2,1)S(1)} %collective-permute-done.2.refs_3_, ...), custom_call_target="tpu_custom_call" | custom-call | tf_op jit(solution)/shard_map/gram/pallas_call | solution.py:327
  28.1 0.0 copy-start
  28.1 0.1 collective-permute-start.12
  28.2 2.1 %collective-permute-done.12.other = f32[10,128,128]{2,1,0:T(8,128)S(1)} collective-permute-done((f32[10,128,128]{2,1,0:T(8,128)S(1)}, f32[10,128,128]{2,1,0:T(8,128)S(1)}, u32[]{:S(2)}, u32[]{:S(2)}) %collective-permute-start.12) | collective-permute-done | bytes 655392 | tf_op jit(solution)/shard_map/ppermute | solution.py:335
  30.3 0.0 copy-done
  30.3 3.3 %newton.1 = f32[256,512]{1,0:T(8,128)S(1)} custom-call(f32[2,4]{1,0:T(2,128)S(1)} %bitcast.9, f32[10,128,128]{2,1,0:T(8,128)S(1)} %gram.1.mine, f32[10,128,128]{2,1,0:T(8,128)S(1)} %collective-permute-done.12.other), custom_call_target="tpu_custom_call" | custom-call | tf_op jit(solution)/shard_map/newton/pallas_call | solution.py:336
  33.7 0.1 pad_maximum_fusion
  33.8 20.8 %all_to_all.9 = f16[16,32,512]{2,1,0:T(8,128)(2,1)S(1)} all-to-all(f16[16,32,512]{2,1,0:T(8,128)(2,1)S(1)} %bitcast.10), channel_id=1, replica_groups={{0,2,4,6,8,10,12,14,16,18,20,22,24,26,28,30},{1,3,5,7,9,11,13,15,17,19,..., dimensions={0} | all-to-all | bytes 1048576 | tf_op jit(solution)/shard_map/all_to_all | solution.py:350
  54.6 0.1 convert_multiply_fusion
  54.8 1.2 %decode.1 = (f32[8,1,32,512]{3,2,1,0:T(8,128)}, f32[8,1,32,512]{3,2,1,0:T(8,128)}) custom-call(f32[512,512]{1,0:T(8,128)S(1)} %bitcast.8), custom_call_target="tpu_custom_call" | custom-call | tf_op jit(solution)/shard_map/decode/pallas_call | solution.py:354
  (1 shorter events, 0.0 us)
Async XLA Ops:
  1.7 12.4 %collective-permute-start.4 = (bf16[136,512]{1,0:T(8,128)(2,1)S(1)}, bf16[136,512]{1,0:T(8,128)(2,1)S(1)}, u32[]{:S(2)}, u32[]{:S(2)}) collective-permute-start(bf16[136,512]{1,0:T(8,128)(2,1)S(1)} %get-tuple-element.23), channel_id=1, source_target_pairs={{0,8},{1,9},{2,10},{3,11},{4,12},{5,13},{6,14},{7,15},{8,0},{9,1},... | collective-permute-start | bytes 417800 | tf_op jit(solution)/shard_map/ppermute | solution.py:319
  6.2 9.6 %collective-permute-start = (bf16[64,512]{1,0:T(8,128)(2,1)S(1)}, bf16[64,512]{1,0:T(8,128)(2,1)S(1)}, u32[]{:S(2)}, u32[]{:S(2)}) collective-permute-start(bf16[64,512]{1,0:T(8,128)(2,1)S(1)} %get-tuple-element.19), channel_id=1, source_target_pairs={{0,22},{1,23},{2,20},{3,21},{4,18},{5,19},{6,16},{7,17},{8,30},{9,... | collective-permute-start | bytes 196616 | tf_op jit(solution)/shard_map/ppermute | solution.py:315
  9.7 8.0 %collective-permute-start.1 = (bf16[64,512]{1,0:T(8,128)(2,1)S(1)}, bf16[64,512]{1,0:T(8,128)(2,1)S(1)}, u32[]{:S(2)}, u32[]{:S(2)}) collective-permute-start(bf16[64,512]{1,0:T(8,128)(2,1)S(1)} %get-tuple-element.20), channel_id=1, source_target_pairs={{0,6},{1,7},{2,4},{3,5},{4,2},{5,3},{6,0},{7,1},{8,14},{9,15},{10,... | collective-permute-start | bytes 196616 | tf_op jit(solution)/shard_map/ppermute | solution.py:315
  10.1 8.6 %collective-permute-start.2 = (bf16[64,512]{1,0:T(8,128)(2,1)S(1)}, bf16[64,512]{1,0:T(8,128)(2,1)S(1)}, u32[]{:S(2)}, u32[]{:S(2)}) collective-permute-start(bf16[64,512]{1,0:T(8,128)(2,1)S(1)} %get-tuple-element.21), channel_id=1, source_target_pairs={{0,20},{1,21},{2,22},{3,23},{4,16},{5,17},{6,18},{7,19},{8,28},{9,... | collective-permute-start | bytes 196616 | tf_op jit(solution)/shard_map/ppermute | solution.py:315
  11.7 7.7 %collective-permute-start.3 = (bf16[64,512]{1,0:T(8,128)(2,1)S(1)}, bf16[64,512]{1,0:T(8,128)(2,1)S(1)}, u32[]{:S(2)}, u32[]{:S(2)}) collective-permute-start(bf16[64,512]{1,0:T(8,128)(2,1)S(1)} %get-tuple-element.22), channel_id=1, source_target_pairs={{0,18},{1,19},{2,16},{3,17},{4,22},{5,23},{6,20},{7,21},{8,26},{9,... | collective-permute-start | bytes 196616 | tf_op jit(solution)/shard_map/ppermute | solution.py:315
  14.7 6.7 %collective-permute-start.8 = (bf16[64,512]{1,0:T(8,128)(2,1)S(1)}, bf16[64,512]{1,0:T(8,128)(2,1)S(1)}, u32[]{:S(2)}, u32[]{:S(2)}) collective-permute-start(bf16[64,512]{1,0:T(8,128)(2,1)S(1)} %get-tuple-element.28), channel_id=1, source_target_pairs={{0,22},{1,23},{2,20},{3,21},{4,18},{5,19},{6,16},{7,17},{8,30},{9,... | collective-permute-start | bytes 196616 | tf_op jit(solution)/shard_map/ppermute | solution.py:315
  15.8 6.4 %collective-permute-start.9 = (bf16[64,512]{1,0:T(8,128)(2,1)S(1)}, bf16[64,512]{1,0:T(8,128)(2,1)S(1)}, u32[]{:S(2)}, u32[]{:S(2)}) collective-permute-start(bf16[64,512]{1,0:T(8,128)(2,1)S(1)} %get-tuple-element.29), channel_id=1, source_target_pairs={{0,6},{1,7},{2,4},{3,5},{4,2},{5,3},{6,0},{7,1},{8,14},{9,15},{10,... | collective-permute-start | bytes 196616 | tf_op jit(solution)/shard_map/ppermute | solution.py:315
  17.7 9.7 %collective-permute-start.5 = (bf16[128,512]{1,0:T(8,128)(2,1)S(1)}, bf16[128,512]{1,0:T(8,128)(2,1)S(1)}, u32[]{:S(2)}, u32[]{:S(2)}) collective-permute-start(bf16[128,512]{1,0:T(8,128)(2,1)S(1)} %get-tuple-element.25), channel_id=1, source_target_pairs={{0,2},{1,3},{2,0},{3,1},{4,6},{5,7},{6,4},{7,5},{8,10},{9,11},{10,... | collective-permute-start | bytes 393224 | tf_op jit(solution)/shard_map/ppermute | solution.py:315
  18.7 8.7 %collective-permute-start.6 = (bf16[128,512]{1,0:T(8,128)(2,1)S(1)}, bf16[128,512]{1,0:T(8,128)(2,1)S(1)}, u32[]{:S(2)}, u32[]{:S(2)}) collective-permute-start(bf16[128,512]{1,0:T(8,128)(2,1)S(1)} %get-tuple-element.26), channel_id=1, source_target_pairs={{0,4},{1,5},{2,6},{3,7},{4,0},{5,1},{6,2},{7,3},{8,12},{9,13},{10,... | collective-permute-start | bytes 393224 | tf_op jit(solution)/shard_map/ppermute | solution.py:315
  19.3 8.1 %collective-permute-start.7 = (bf16[128,512]{1,0:T(8,128)(2,1)S(1)}, bf16[128,512]{1,0:T(8,128)(2,1)S(1)}, u32[]{:S(2)}, u32[]{:S(2)}) collective-permute-start(bf16[128,512]{1,0:T(8,128)(2,1)S(1)} %get-tuple-element.27), channel_id=1, source_target_pairs={{0,16},{1,17},{2,18},{3,19},{4,20},{5,21},{6,22},{7,23},{8,24},{9,... | collective-permute-start | bytes 393224 | tf_op jit(solution)/shard_map/ppermute | solution.py:315
  21.5 5.2 %collective-permute-start.10 = (bf16[64,512]{1,0:T(8,128)(2,1)S(1)}, bf16[64,512]{1,0:T(8,128)(2,1)S(1)}, u32[]{:S(2)}, u32[]{:S(2)}) collective-permute-start(bf16[64,512]{1,0:T(8,128)(2,1)S(1)} %get-tuple-element.30), channel_id=1, source_target_pairs={{0,20},{1,21},{2,22},{3,23},{4,16},{5,17},{6,18},{7,19},{8,28},{9,... | collective-permute-start | bytes 196616 | tf_op jit(solution)/shard_map/ppermute | solution.py:315
  22.2 5.2 %collective-permute-start.11 = (bf16[64,512]{1,0:T(8,128)(2,1)S(1)}, bf16[64,512]{1,0:T(8,128)(2,1)S(1)}, u32[]{:S(2)}, u32[]{:S(2)}) collective-permute-start(bf16[64,512]{1,0:T(8,128)(2,1)S(1)} %get-tuple-element.31), channel_id=1, source_target_pairs={{0,18},{1,19},{2,16},{3,17},{4,22},{5,23},{6,20},{7,21},{8,26},{9,... | collective-permute-start | bytes 196616 | tf_op jit(solution)/shard_map/ppermute | solution.py:315
  28.1 2.2 %copy-start = (f32[4,2,1]{0,2,1:T(1,128)S(1)}, f32[4,2,1]{0,2,1:T(1,128)}, u32[]{:S(2)}) copy-start(f32[4,2,1]{0,2,1:T(1,128)} %param.11) | copy-start | bytes 100
  28.1 2.2 %collective-permute-start.12 = (f32[10,128,128]{2,1,0:T(8,128)S(1)}, f32[10,128,128]{2,1,0:T(8,128)S(1)}, u32[]{:S(2)}, u32[]{:S(2)}) collective-permute-start(f32[10,128,128]{2,1,0:T(8,128)S(1)} %gram.1.mine), channel_id=1, source_target_pairs={{0,1},{1,0},{2,3},{3,2},{4,5},{5,4},{6,7},{7,6},{8,9},{9,8},{10,11... | collective-permute-start | bytes 1966088 | tf_op jit(solution)/shard_map/ppermute | solution.py:335

commit v2 on v1

--- a/solution.py
+++ b/solution.py
@@ -136,15 +136,17 @@
             outputs[index][row : row + CAP, :] = rows[rank * CAP : (rank + 1) * CAP]
 
 
-def gram_kernel(*refs):
-    rows = jnp.concatenate([ref[...] for ref in refs[:-1]], axis=0)
+def gram_kernel(blocks, *refs):
+    inputs, before, out = refs[:blocks], refs[blocks:-1], refs[-1]
+    rows = jnp.concatenate([ref[...] for ref in inputs], axis=0)
     gram = lax.dot_general(
         rows, rows, (((0,), (0,)), ((), ())), preferred_element_type=jnp.float32
     )
     for index, (top, left) in enumerate(UPPER):
-        refs[-1][index] = gram[
-            top * LANES : (top + 1) * LANES, left * LANES : (left + 1) * LANES
-        ]
+        tile = gram[top * LANES : (top + 1) * LANES, left * LANES : (left + 1) * LANES]
+        for ref in before:
+            tile = tile + ref[index]
+        out[index] = tile
 
 
 def split(value):
@@ -322,16 +324,22 @@
     for block, (step, _) in zip(blocks, early):
         received.append(deliver(block, step))
     blocks = pack([own, got], late)
+    last = []
     for block, (step, _) in zip(blocks, late):
-        received.append(deliver(block, step))
-    mine = pl.pallas_call(
-        gram_kernel,
-        out_shape=pltpu.VMEM((len(UPPER), LANES, LANES), jnp.float32),
-        in_specs=[spec] * len(received),
-        out_specs=spec,
-        compiler_params=params,
-        name="gram",
-    )(*received)
+        (last if step in EARLY[1:] else received).append(deliver(block, step))
+
+    def gram(blocks, *before):
+        return pl.pallas_call(
+            functools.partial(gram_kernel, len(blocks)),
+            out_shape=pltpu.VMEM((len(UPPER), LANES, LANES), jnp.float32),
+            in_specs=[spec] * (len(blocks) + len(before)),
+            out_specs=spec,
+            compiler_params=params,
+            name="gram",
+        )(*blocks, *before)
+
+    partial = gram(received)
+    mine = gram(last, partial)
     other = lax.ppermute(mine, "dp", [(i, i ^ 1) for i in range(shards)])
     rows = pl.pallas_call(
         functools.partial(newton_kernel, load_inverse, owners, shards),

time: 56.2 us -> 60.6 us (1.078)
  waiting for transfers between devices: 6.59 us -> 10.3 us
    ppermute x1, waiting for transfers between devices: 0.01 us -> 2.46 us  [owned(): lax.ppermute(sent, 'dp', [(i, (i + far) % shards) for i in range(shards)])]
    ppermute x11, waiting for transfers between devices: 4.51 us -> 5.79 us  [deliver(): return lax.ppermute(block, AXES, [(i, i ^ apart) for i in range(devices)])]
  transfers between devices with their start and end apart: 13 -> 13, of which waited for: 4 -> 7; matrix products, arithmetic and copies ran while one was open for 0% -> 0% of each run, Pallas kernels for 2% -> 3%
where the time goes in v2:
time: 60.6 us; the launch traced here: 60.4 us
  blocking collectives  21.1 us (35%)
  starting transfers between devices  20.5 us (34%)
  waiting for transfers between devices  10.3 us (17%)
  Pallas kernels  7.46 us (12%)
  between operations  0.73 us (1%)
    all_to_all x1, blocking collectives, owned(): lax.all_to_all(sent, AXES, split_axis=0, concat_axis=0, tiled=True, axis_...  21.1 us
    ppermute x11, starting transfers between devices, deliver(): return lax.ppermute(block, AXES, [(i, i ^ apart) for i in range(devices)])  16.3 us
    ppermute x11, waiting for transfers between devices, deliver(): return lax.ppermute(block, AXES, [(i, i ^ apart) for i in range(devices)])  5.79 us
    ppermute x1, starting transfers between devices, owned(): lax.ppermute(sent, 'dp', [(i, (i + far) % shards) for i in range(shards)])  4.13 us
    pallas_call x1, Pallas kernels, owned(): pl.pallas_call(functools.partial(newton_kernel, load_inverse, owners, sha...  3.29 us
    ppermute x1, waiting for transfers between devices, owned(): lax.ppermute(sent, 'dp', [(i, (i + far) % shards) for i in range(shards)])  2.46 us
    ppermute x1, waiting for transfers between devices, owned(): other = lax.ppermute(mine, 'dp', [(i, i ^ 1) for i in range(shards)])  2.08 us
    pallas_call x1, Pallas kernels, owned(): pl.pallas_call(decode_kernel, out_shape=(result, result), in_specs=[spec]...  1.22 us
  transfers between devices with their start and end apart: 13, of which 7 were waited for; matrix products, arithmetic and copies ran while one was open for 0% of the time, Pallas kernels for 3%

profile of v2, /device:TPU:0, one launch (start us, length us, event | category | flops | bytes accessed | tf_op | source)
XLA Modules:
  0.0 60.4 jit_solution(9601958658277917532)
XLA Ops:
  0.6 1.1 %collect.1 = (bf16[136,512]{1,0:T(8,128)(2,1)S(1)}, bf16[136,512]{1,0:T(8,128)(2,1)S(1)}) custom-call(bf16[128,512]{1,0:T(8,128)(2,1)} %features.1, bf16[128,512]{1,0:T(8,128)(2,1)} %gradients.1, s32[2,128]{1,0:T(2,128)} %bitcast.11, f32[1,128]{1,0:T(1,128)} %bitcast.12, s32[1,128]{1,0:T(1,128)} %bitcast.13), custom_call_target="tpu_custom_call" | custom-call | tf_op jit(solution)/shard_map/collect/pallas_call | solution.py:275
  1.7 4.1 %collective-permute-start = (bf16[136,512]{1,0:T(8,128)(2,1)S(1)}, bf16[136,512]{1,0:T(8,128)(2,1)S(1)}, u32[]{:S(2)}, u32[]{:S(2)}) collective-permute-start(bf16[136,512]{1,0:T(8,128)(2,1)S(1)} %get-tuple-element.18), channel_id=1, source_target_pairs={{0,8},{1,9},{2,10},{3,11},{4,12},{5,13},{6,14},{7,15},{8,0},{9,1},... | collective-permute-start | bytes 417800 | tf_op jit(solution)/shard_map/ppermute | solution.py:321
  5.8 0.4 pack.3
  6.2 3.5 %collective-permute-start.5 = (bf16[64,512]{1,0:T(8,128)(2,1)S(1)}, bf16[64,512]{1,0:T(8,128)(2,1)S(1)}, u32[]{:S(2)}, u32[]{:S(2)}) collective-permute-start(bf16[64,512]{1,0:T(8,128)(2,1)S(1)} %get-tuple-element.24), channel_id=1, source_target_pairs={{0,22},{1,23},{2,20},{3,21},{4,18},{5,19},{6,16},{7,17},{8,30},{9,... | collective-permute-start | bytes 196616 | tf_op jit(solution)/shard_map/ppermute | solution.py:317
  9.7 0.4 collective-permute-start.6
  10.1 2.5 %collective-permute-done.refs_1_ = bf16[136,512]{1,0:T(8,128)(2,1)S(1)} collective-permute-done((bf16[136,512]{1,0:T(8,128)(2,1)S(1)}, bf16[136,512]{1,0:T(8,128)(2,1)S(1)}, u32[]{:S(2)}, u32[]{:S(2)}) %collective-permute-start) | collective-permute-done | bytes 139296 | tf_op jit(solution)/shard_map/ppermute | solution.py:321
  12.6 0.6 %pack.2 = (bf16[64,512]{1,0:T(8,128)(2,1)S(1)}, bf16[128,512]{1,0:T(8,128)(2,1)S(1)}, bf16[128,512]{1,0:T(8,128)(2,1)S(1)}, bf16[128,512]{1,0:T(8,128)(2,1)S(1)}...) custom-call(bf16[136,512]{1,0:T(8,128)(2,1)S(1)} %get-tuple-element., ...), custom_call_target="tpu_custom_call" | custom-call | tf_op jit(solution)/shard_map/pack/pallas_call | solution.py:304
  13.2 1.6 %collective-permute-start.9 = (bf16[128,512]{1,0:T(8,128)(2,1)S(1)}, bf16[128,512]{1,0:T(8,128)(2,1)S(1)}, u32[]{:S(2)}, u32[]{:S(2)}) collective-permute-start(bf16[128,512]{1,0:T(8,128)(2,1)S(1)} %get-tuple-element.29), channel_id=1, source_target_pairs={{0,2},{1,3},{2,0},{3,1},{4,6},{5,7},{6,4},{7,5},{8,10},{9,11},{10,... | collective-permute-start | bytes 393224 | tf_op jit(solution)/shard_map/ppermute | solution.py:317
  14.8 0.6 %collective-permute-start.10 = (bf16[128,512]{1,0:T(8,128)(2,1)S(1)}, bf16[128,512]{1,0:T(8,128)(2,1)S(1)}, u32[]{:S(2)}, u32[]{:S(2)}) collective-permute-start(bf16[128,512]{1,0:T(8,128)(2,1)S(1)} %get-tuple-element.30), channel_id=1, source_target_pairs={{0,4},{1,5},{2,6},{3,7},{4,0},{5,1},{6,2},{7,3},{8,12},{9,13},{10,... | collective-permute-start | bytes 393224 | tf_op jit(solution)/shard_map/ppermute | solution.py:317
  15.5 2.3 %collective-permute-start.7 = (bf16[64,512]{1,0:T(8,128)(2,1)S(1)}, bf16[64,512]{1,0:T(8,128)(2,1)S(1)}, u32[]{:S(2)}, u32[]{:S(2)}) collective-permute-start(bf16[64,512]{1,0:T(8,128)(2,1)S(1)} %get-tuple-element.26), channel_id=1, source_target_pairs={{0,20},{1,21},{2,22},{3,23},{4,16},{5,17},{6,18},{7,19},{8,28},{9,... | collective-permute-start | bytes 196616 | tf_op jit(solution)/shard_map/ppermute | solution.py:317
  17.8 0.0 collective-permute-done.5.refs_1_
  17.8 0.4 collective-permute-start.8
  18.2 0.0 collective-permute-done.6.refs_2_
  18.2 1.5 %collective-permute-start.11 = (bf16[128,512]{1,0:T(8,128)(2,1)S(1)}, bf16[128,512]{1,0:T(8,128)(2,1)S(1)}, u32[]{:S(2)}, u32[]{:S(2)}) collective-permute-start(bf16[128,512]{1,0:T(8,128)(2,1)S(1)} %get-tuple-element.31), channel_id=1, source_target_pairs={{0,16},{1,17},{2,18},{3,19},{4,20},{5,21},{6,22},{7,23},{8,24},{9,... | collective-permute-start | bytes 393224 | tf_op jit(solution)/shard_map/ppermute | solution.py:317
  19.8 1.8 %collective-permute-done.7.refs_3_ = bf16[64,512]{1,0:T(8,128)(2,1)S(1)} collective-permute-done((bf16[64,512]{1,0:T(8,128)(2,1)S(1)}, bf16[64,512]{1,0:T(8,128)(2,1)S(1)}, u32[]{:S(2)}, u32[]{:S(2)}) %collective-permute-start.7) | collective-permute-done | bytes 65568 | tf_op jit(solution)/shard_map/ppermute | solution.py:317
  21.5 1.4 %collective-permute-start.1 = (bf16[64,512]{1,0:T(8,128)(2,1)S(1)}, bf16[64,512]{1,0:T(8,128)(2,1)S(1)}, u32[]{:S(2)}, u32[]{:S(2)}) collective-permute-start(bf16[64,512]{1,0:T(8,128)(2,1)S(1)} %get-tuple-element.19), channel_id=1, source_target_pairs={{0,22},{1,23},{2,20},{3,21},{4,18},{5,19},{6,16},{7,17},{8,30},{9,... | collective-permute-start | bytes 196616 | tf_op jit(solution)/shard_map/ppermute | solution.py:317
  23.0 0.0 collective-permute-done.8.refs_4_
  23.0 2.1 %collective-permute-start.2 = (bf16[64,512]{1,0:T(8,128)(2,1)S(1)}, bf16[64,512]{1,0:T(8,128)(2,1)S(1)}, u32[]{:S(2)}, u32[]{:S(2)}) collective-permute-start(bf16[64,512]{1,0:T(8,128)(2,1)S(1)} %get-tuple-element.20), channel_id=1, source_target_pairs={{0,6},{1,7},{2,4},{3,5},{4,2},{5,3},{6,0},{7,1},{8,14},{9,15},{10,... | collective-permute-start | bytes 196616 | tf_op jit(solution)/shard_map/ppermute | solution.py:317
  25.1 0.0 collective-permute-done.9.refs_6_
  25.1 1.7 %collective-permute-start.3 = (bf16[64,512]{1,0:T(8,128)(2,1)S(1)}, bf16[64,512]{1,0:T(8,128)(2,1)S(1)}, u32[]{:S(2)}, u32[]{:S(2)}) collective-permute-start(bf16[64,512]{1,0:T(8,128)(2,1)S(1)} %get-tuple-element.21), channel_id=1, source_target_pairs={{0,20},{1,21},{2,22},{3,23},{4,16},{5,17},{6,18},{7,19},{8,28},{9,... | collective-permute-start | bytes 196616 | tf_op jit(solution)/shard_map/ppermute | solution.py:317
  26.8 0.0 collective-permute-done.10.refs_7_
  26.8 0.6 collective-permute-start.4
  27.4 0.0 collective-permute-done.11.refs_8_
  27.4 0.6 gram.2.refs_4_
  28.0 0.1 collective-permute-done.1.refs_0_
  28.1 0.6 collective-permute-done.2.refs_1_
  28.7 1.6 %collective-permute-done.3.refs_2_ = bf16[64,512]{1,0:T(8,128)(2,1)S(1)} collective-permute-done((bf16[64,512]{1,0:T(8,128)(2,1)S(1)}, bf16[64,512]{1,0:T(8,128)(2,1)S(1)}, u32[]{:S(2)}, u32[]{:S(2)}) %collective-permute-start.3) | collective-permute-done | bytes 65568 | tf_op jit(solution)/shard_map/ppermute | solution.py:317
  30.3 1.7 %collective-permute-done.4.refs_3_ = bf16[64,512]{1,0:T(8,128)(2,1)S(1)} collective-permute-done((bf16[64,512]{1,0:T(8,128)(2,1)S(1)}, bf16[64,512]{1,0:T(8,128)(2,1)S(1)}, u32[]{:S(2)}, u32[]{:S(2)}) %collective-permute-start.4) | collective-permute-done | bytes 65568 | tf_op jit(solution)/shard_map/ppermute | solution.py:317
  32.0 0.3 gram.3.mine
  32.3 0.0 copy-start
  32.3 0.1 collective-permute-start.12
  32.4 2.1 %collective-permute-done.12.other = f32[10,128,128]{2,1,0:T(8,128)S(1)} collective-permute-done((f32[10,128,128]{2,1,0:T(8,128)S(1)}, f32[10,128,128]{2,1,0:T(8,128)S(1)}, u32[]{:S(2)}, u32[]{:S(2)}) %collective-permute-start.12) | collective-permute-done | bytes 655392 | tf_op jit(solution)/shard_map/ppermute | solution.py:343
  34.5 0.0 copy-done
  34.5 3.3 %newton.1 = f32[256,512]{1,0:T(8,128)S(1)} custom-call(f32[2,4]{1,0:T(2,128)S(1)} %bitcast.9, f32[10,128,128]{2,1,0:T(8,128)S(1)} %gram.3.mine, f32[10,128,128]{2,1,0:T(8,128)S(1)} %collective-permute-done.12.other), custom_call_target="tpu_custom_call" | custom-call | tf_op jit(solution)/shard_map/newton/pallas_call | solution.py:344
  37.8 0.1 pad_maximum_fusion
  38.0 21.1 %all_to_all.9 = f16[16,32,512]{2,1,0:T(8,128)(2,1)S(1)} all-to-all(f16[16,32,512]{2,1,0:T(8,128)(2,1)S(1)} %bitcast.10), channel_id=1, replica_groups={{0,2,4,6,8,10,12,14,16,18,20,22,24,26,28,30},{1,3,5,7,9,11,13,15,17,19,..., dimensions={0} | all-to-all | bytes 1048576 | tf_op jit(solution)/shard_map/all_to_all | solution.py:358
  59.0 0.1 convert_multiply_fusion
  59.2 1.2 %decode.1 = (f32[8,1,32,512]{3,2,1,0:T(8,128)}, f32[8,1,32,512]{3,2,1,0:T(8,128)}) custom-call(f32[512,512]{1,0:T(8,128)S(1)} %bitcast.8), custom_call_target="tpu_custom_call" | custom-call | tf_op jit(solution)/shard_map/decode/pallas_call | solution.py:362
  (1 shorter events, 0.0 us)
Async XLA Ops:
  1.7 10.9 %collective-permute-start = (bf16[136,512]{1,0:T(8,128)(2,1)S(1)}, bf16[136,512]{1,0:T(8,128)(2,1)S(1)}, u32[]{:S(2)}, u32[]{:S(2)}) collective-permute-start(bf16[136,512]{1,0:T(8,128)(2,1)S(1)} %get-tuple-element.18), channel_id=1, source_target_pairs={{0,8},{1,9},{2,10},{3,11},{4,12},{5,13},{6,14},{7,15},{8,0},{9,1},... | collective-permute-start | bytes 417800 | tf_op jit(solution)/shard_map/ppermute | solution.py:321
  6.2 11.6 %collective-permute-start.5 = (bf16[64,512]{1,0:T(8,128)(2,1)S(1)}, bf16[64,512]{1,0:T(8,128)(2,1)S(1)}, u32[]{:S(2)}, u32[]{:S(2)}) collective-permute-start(bf16[64,512]{1,0:T(8,128)(2,1)S(1)} %get-tuple-element.24), channel_id=1, source_target_pairs={{0,22},{1,23},{2,20},{3,21},{4,18},{5,19},{6,16},{7,17},{8,30},{9,... | collective-permute-start | bytes 196616 | tf_op jit(solution)/shard_map/ppermute | solution.py:317
  9.7 8.5 %collective-permute-start.6 = (bf16[64,512]{1,0:T(8,128)(2,1)S(1)}, bf16[64,512]{1,0:T(8,128)(2,1)S(1)}, u32[]{:S(2)}, u32[]{:S(2)}) collective-permute-start(bf16[64,512]{1,0:T(8,128)(2,1)S(1)} %get-tuple-element.25), channel_id=1, source_target_pairs={{0,6},{1,7},{2,4},{3,5},{4,2},{5,3},{6,0},{7,1},{8,14},{9,15},{10,... | collective-permute-start | bytes 196616 | tf_op jit(solution)/shard_map/ppermute | solution.py:317
  13.2 11.9 %collective-permute-start.9 = (bf16[128,512]{1,0:T(8,128)(2,1)S(1)}, bf16[128,512]{1,0:T(8,128)(2,1)S(1)}, u32[]{:S(2)}, u32[]{:S(2)}) collective-permute-start(bf16[128,512]{1,0:T(8,128)(2,1)S(1)} %get-tuple-element.29), channel_id=1, source_target_pairs={{0,2},{1,3},{2,0},{3,1},{4,6},{5,7},{6,4},{7,5},{8,10},{9,11},{10,... | collective-permute-start | bytes 393224 | tf_op jit(solution)/shard_map/ppermute | solution.py:317
  14.8 12.0 %collective-permute-start.10 = (bf16[128,512]{1,0:T(8,128)(2,1)S(1)}, bf16[128,512]{1,0:T(8,128)(2,1)S(1)}, u32[]{:S(2)}, u32[]{:S(2)}) collective-permute-start(bf16[128,512]{1,0:T(8,128)(2,1)S(1)} %get-tuple-element.30), channel_id=1, source_target_pairs={{0,4},{1,5},{2,6},{3,7},{4,0},{5,1},{6,2},{7,3},{8,12},{9,13},{10,... | collective-permute-start | bytes 393224 | tf_op jit(solution)/shard_map/ppermute | solution.py:317
  15.5 6.1 %collective-permute-start.7 = (bf16[64,512]{1,0:T(8,128)(2,1)S(1)}, bf16[64,512]{1,0:T(8,128)(2,1)S(1)}, u32[]{:S(2)}, u32[]{:S(2)}) collective-permute-start(bf16[64,512]{1,0:T(8,128)(2,1)S(1)} %get-tuple-element.26), channel_id=1, source_target_pairs={{0,20},{1,21},{2,22},{3,23},{4,16},{5,17},{6,18},{7,19},{8,28},{9,... | collective-permute-start | bytes 196616 | tf_op jit(solution)/shard_map/ppermute | solution.py:317
  17.8 5.2 %collective-permute-start.8 = (bf16[64,512]{1,0:T(8,128)(2,1)S(1)}, bf16[64,512]{1,0:T(8,128)(2,1)S(1)}, u32[]{:S(2)}, u32[]{:S(2)}) collective-permute-start(bf16[64,512]{1,0:T(8,128)(2,1)S(1)} %get-tuple-element.27), channel_id=1, source_target_pairs={{0,18},{1,19},{2,16},{3,17},{4,22},{5,23},{6,20},{7,21},{8,26},{9,... | collective-permute-start | bytes 196616 | tf_op jit(solution)/shard_map/ppermute | solution.py:317
  18.2 9.2 %collective-permute-start.11 = (bf16[128,512]{1,0:T(8,128)(2,1)S(1)}, bf16[128,512]{1,0:T(8,128)(2,1)S(1)}, u32[]{:S(2)}, u32[]{:S(2)}) collective-permute-start(bf16[128,512]{1,0:T(8,128)(2,1)S(1)} %get-tuple-element.31), channel_id=1, source_target_pairs={{0,16},{1,17},{2,18},{3,19},{4,20},{5,21},{6,22},{7,23},{8,24},{9,... | collective-permute-start | bytes 393224 | tf_op jit(solution)/shard_map/ppermute | solution.py:317
  21.5 6.6 %collective-permute-start.1 = (bf16[64,512]{1,0:T(8,128)(2,1)S(1)}, bf16[64,512]{1,0:T(8,128)(2,1)S(1)}, u32[]{:S(2)}, u32[]{:S(2)}) collective-permute-start(bf16[64,512]{1,0:T(8,128)(2,1)S(1)} %get-tuple-element.19), channel_id=1, source_target_pairs={{0,22},{1,23},{2,20},{3,21},{4,18},{5,19},{6,16},{7,17},{8,30},{9,... | collective-permute-start | bytes 196616 | tf_op jit(solution)/shard_map/ppermute | solution.py:317
  23.0 5.7 %collective-permute-start.2 = (bf16[64,512]{1,0:T(8,128)(2,1)S(1)}, bf16[64,512]{1,0:T(8,128)(2,1)S(1)}, u32[]{:S(2)}, u32[]{:S(2)}) collective-permute-start(bf16[64,512]{1,0:T(8,128)(2,1)S(1)} %get-tuple-element.20), channel_id=1, source_target_pairs={{0,6},{1,7},{2,4},{3,5},{4,2},{5,3},{6,0},{7,1},{8,14},{9,15},{10,... | collective-permute-start | bytes 196616 | tf_op jit(solution)/shard_map/ppermute | solution.py:317
  25.1 5.2 %collective-permute-start.3 = (bf16[64,512]{1,0:T(8,128)(2,1)S(1)}, bf16[64,512]{1,0:T(8,128)(2,1)S(1)}, u32[]{:S(2)}, u32[]{:S(2)}) collective-permute-start(bf16[64,512]{1,0:T(8,128)(2,1)S(1)} %get-tuple-element.21), channel_id=1, source_target_pairs={{0,20},{1,21},{2,22},{3,23},{4,16},{5,17},{6,18},{7,19},{8,28},{9,... | collective-permute-start | bytes 196616 | tf_op jit(solution)/shard_map/ppermute | solution.py:317
  26.8 5.2 %collective-permute-start.4 = (bf16[64,512]{1,0:T(8,128)(2,1)S(1)}, bf16[64,512]{1,0:T(8,128)(2,1)S(1)}, u32[]{:S(2)}, u32[]{:S(2)}) collective-permute-start(bf16[64,512]{1,0:T(8,128)(2,1)S(1)} %get-tuple-element.22), channel_id=1, source_target_pairs={{0,18},{1,19},{2,16},{3,17},{4,22},{5,23},{6,20},{7,21},{8,26},{9,... | collective-permute-start | bytes 196616 | tf_op jit(solution)/shard_map/ppermute | solution.py:317
  32.3 2.2 %copy-start = (f32[4,2,1]{0,2,1:T(1,128)S(1)}, f32[4,2,1]{0,2,1:T(1,128)}, u32[]{:S(2)}) copy-start(f32[4,2,1]{0,2,1:T(1,128)} %param.11) | copy-start | bytes 100
  32.3 2.2 %collective-permute-start.12 = (f32[10,128,128]{2,1,0:T(8,128)S(1)}, f32[10,128,128]{2,1,0:T(8,128)S(1)}, u32[]{:S(2)}, u32[]{:S(2)}) collective-permute-start(f32[10,128,128]{2,1,0:T(8,128)S(1)} %gram.3.mine), channel_id=1, source_target_pairs={{0,1},{1,0},{2,3},{3,2},{4,5},{5,4},{6,7},{7,6},{8,9},{9,8},{10,11... | collective-permute-start | bytes 1966088 | tf_op jit(solution)/shard_map/ppermute | solution.py:343
